TPU v7x, 32 devices: a whole 2x2x4 slice. The times are simulated.
32 devices in a mesh: fsdp: 16 (over z, y, x), tp: 2 (over core).
Axes of the slice: x: 2, y: 2, z: 4, core: 2. Of those that a mesh axis runs over, the one named last changes fastest.
Arguments:
- inputs: bfloat16 [4096, 4096], P('fsdp'), may hold values from -6 to 6
- value_grad: bfloat16 [4096, 1024], P('fsdp', 'tp'), may hold values from -24 to 24
- value_weight: bfloat16 [4096, 1024], P('tp', 'fsdp'), may hold values from -0.09375 to 0.09375
- counts: int32 [16, 4], P('fsdp'), may hold values from 1 to 232, as said below
- offsets: int32 [16, 4], P('fsdp'), may hold values from 0 to 248, as said below
Outputs:
- input_grad: bfloat16 [4096, 4096], P('fsdp', 'tp')
- weight_grad: float32 [4096, 1024], P('fsdp', 'tp')
Inputs may be any that keep to these rules, and one draw needn't show every extreme that they name: `offsets`: on each index of fsdp the 4 samples lie in order; each starts at a multiple of 8, at or after the 8-row-aligned end of the previous one, and all lie within the 256 rows; on some index the aligned blocks of its samples fill all 256 rows. `counts`: how many rows the samples of a row group fill varies widely between indices of fsdp.
All inputs are finite; a program needn't handle non-finite values.
Results may differ from a plain program's by a relative error of at most 0.0046.
Values may be sent and summed in bfloat16 or wider, within the bound.
A program may use at most 64 MiB of HBM per device.

v0:
```python
import functools
import math

import jax
import jax.numpy as jnp
from jax import lax
from jax.experimental import pallas as pl
from jax.experimental.pallas import tpu as pltpu
from jax.sharding import PartitionSpec as P

MESH = pl.DeviceIdType.MESH
GROUP = 4
VMEM_ROOM = 58 * 2**20


def scale_rows(value_grad, counts, offsets):
    positions = jnp.arange(value_grad.shape[0], dtype=jnp.int32)[:, None]
    starts = offsets[0][None, :]
    lengths = counts[0][None, :]
    inside = (positions >= starts) & (positions < starts + lengths)
    inverse_root = lax.rsqrt(lengths.astype(jnp.float32))
    row_factor = jnp.sum(jnp.where(inside, inverse_root, jnp.zeros_like(inverse_root)), axis=1)
    return (value_grad.astype(jnp.float32) * row_factor[:, None]).astype(jnp.bfloat16)


def general(inputs, value_grad, value_weight, counts, offsets):
    tok_rows = inputs.shape[0]
    row_block = min(128, tok_rows)
    scaled = scale_rows(value_grad, counts, offsets)
    live_end = jnp.max(offsets[0] + counts[0])
    live_blocks = (live_end + row_block - 1) // row_block
    scaled_all = lax.all_gather(scaled, "tp", axis=1, tiled=True)
    empty_inputs = jnp.zeros((tok_rows, value_weight.shape[0]), jnp.float32)
    piece = lax.all_gather(value_weight, "fsdp", axis=1, tiled=True)

    def add_add_block(block_index, partial_value):
        lower = lax.dynamic_slice_in_dim(scaled_all, block_index * row_block, row_block, 0)
        before = lax.dynamic_slice_in_dim(partial_value, block_index * row_block, row_block, 0)
        product = lax.dot_general(
            lower, piece, (((1,), (1,)), ((), ())), preferred_element_type=jnp.float32
        )
        return lax.dynamic_update_slice_in_dim(
            partial_value, before + product, block_index * row_block, 0
        )

    result = lax.fori_loop(0, live_blocks, add_add_block, empty_inputs)
    input_grad = result.astype(jnp.bfloat16)
    normalizer = 1.0 / math.sqrt(counts.shape[1] * lax.axis_size("fsdp"))
    empty = jnp.zeros((inputs.shape[1], scaled.shape[1]), jnp.float32)

    def weight_add_block(block_index, partial_value):
        feature_rows = lax.dynamic_slice_in_dim(inputs, block_index * row_block, row_block, 0)
        grad_rows = lax.dynamic_slice_in_dim(scaled, block_index * row_block, row_block, 0)
        return partial_value + lax.dot_general(
            feature_rows, grad_rows, (((0,), (0,)), ((), ())), preferred_element_type=jnp.float32
        )

    result = lax.fori_loop(0, live_blocks, weight_add_block, empty)
    summed = lax.psum_scatter(result, "fsdp", scatter_dimension=0, tiled=True)
    return (input_grad, summed * normalizer)


def kernel(
    n, normalizer, counts_ref, offsets_ref, x_hbm, g_hbm, wt_hbm, dx_ref, dw_ref,
    x_ref, g_ref, wt_ref, s_ref, s_own, s_sib, x_all, w_all, part_own, part_out, part_in,
    swap_out, swap_in, dx_out, dx_in,
    local_sem, w_send, w_recv, s_send, s_recv, c_send, c_recv, x_send, x_recv,
    g_send, g_recv, p_send, p_recv, o_send, o_recv, swap_send, swap_recv,
):
    nz = n // GROUP
    me = lax.axis_index("fsdp")
    core = lax.axis_index("tp")
    sib = 1 - core
    z = me // GROUP
    quarter = me % GROUP
    dx = 1 - 2 * (me % 2)
    dy = 2 - 4 * ((me // 2) % 2)
    steps = (0, dx, dy, dx + dy)
    tok, half = s_ref.shape
    wcols = wt_ref.shape[0]
    fq = w_all.shape[1]
    zrows = GROUP * wcols
    hr = x_all.shape[2]
    upper = (2 * z) // nz
    order = [a + upper * (nz - 1 - 2 * a) for a in
             list(range(nz - 1, nz // 2 - 1, -1)) + list(range(nz // 2))]

    fetch_g = pltpu.make_async_copy(g_hbm, g_ref, local_sem.at[0])
    fetch_w = pltpu.make_async_copy(wt_hbm, wt_ref, local_sem.at[1])
    fetch_x = pltpu.make_async_copy(x_hbm, x_ref, local_sem.at[2])
    for fetch in (fetch_g, fetch_w, fetch_x):
        fetch.start()

    def remote(src, dst, send, recv, dev):
        return pltpu.make_async_remote_copy(
            src_ref=src, dst_ref=dst, send_sem=send, recv_sem=recv,
            device_id=dev, device_id_type=MESH,
        )

    barrier = pltpu.get_barrier_semaphore()
    for j in range(1, GROUP):
        pl.semaphore_signal(barrier, inc=1, device_id=(me + steps[j], core), device_id_type=MESH)
    pl.semaphore_signal(barrier, inc=1, device_id=(me, sib), device_id_type=MESH)
    ways = ((0, 1, z < nz - 1, z > 0), (1, -1, z > 0, z < nz - 1))
    for side, way, onward, behind in ways:
        @pl.when(onward)
        def _():
            pl.semaphore_signal(barrier, inc=1, device_id=(me + GROUP * way, core), device_id_type=MESH)

    fetch_g.wait()
    positions = lax.broadcasted_iota(jnp.int32, (tok, 128), 0)
    factor = jnp.zeros((tok, 128), jnp.float32)
    for i in range(counts_ref.shape[1]):
        start = jnp.full((tok, 128), offsets_ref[0, i], jnp.int32)
        length = jnp.full((tok, 128), counts_ref[0, i], jnp.int32)
        inside = (positions >= start) & (positions < start + length)
        factor += jnp.where(inside, lax.rsqrt(length.astype(jnp.float32)), 0.0)
    for i in range(half // 128):
        cols = slice(i * 128, (i + 1) * 128)
        scaled = (g_ref[:, cols].astype(jnp.float32) * factor).astype(jnp.bfloat16)
        s_ref[:, cols] = scaled
        s_own[0:tok, cols] = scaled
    fetch_w.wait()

    inner = (z > 0) & (z < nz - 1)

    @pl.when(inner)
    def _():
        pl.semaphore_wait(barrier, GROUP + 2)

    @pl.when(jnp.logical_not(inner))
    def _():
        pl.semaphore_wait(barrier, GROUP + 1)

    def w_rows(f):
        return pl.ds(pl.multiple_of(f * wcols, wcols), wcols)

    def lanes(start, size):
        return pl.ds(pl.multiple_of(start, 128), size)

    def slot(j):
        return pl.ds(j * tok, tok)

    w_copies, s_copies, x_copies = {}, {}, {}
    for j in (3, 1, 2):
        w_copies[j] = remote(
            wt_ref.at[:, lanes((quarter + steps[j]) * fq, fq)], w_all.at[w_rows(me), :],
            w_send.at[j], w_recv.at[j], (me + steps[j], core))
        w_copies[j].start()
    for j in (1, 2):
        s_copies[j] = remote(
            s_ref, s_own.at[slot(j), :], s_send.at[j], s_recv.at[j], (me + steps[j], core))
        s_copies[j].start()
    core_copies = [remote(s_ref, s_sib.at[slot(0), :], c_send.at[0], c_recv.at[0], (me, sib))]
    core_copies[0].start()
    fetch_x.wait()

    def x_lanes(i, q):
        return lanes(((order[i] * GROUP + q) * 2 + core) * hr, hr)

    def x_start(i):
        for j in (3, 1, 2):
            x_copies[i, j] = remote(
                x_ref.at[:, x_lanes(i, quarter + steps[j])], x_all.at[i, slot(j), :],
                x_send.at[i, j], x_recv.at[i, j], (me + steps[j], core))
            x_copies[i, j].start()

    x_start(0)
    w_all[w_rows(me), :] = wt_ref[:, lanes(quarter * fq, fq)]
    for i in range(nz):
        x_all[i, slot(0), :] = x_ref[:, x_lanes(i, quarter)]

    def chain(origin, way, k, h):
        rows = pl.ds(pl.multiple_of(origin * zrows + h * (zrows // 2), zrows // 2), zrows // 2)
        dev = (me + GROUP * way, core)
        return remote(w_all.at[rows, :], w_all.at[rows, :],
                      g_send.at[(1 - way) // 2, k, h], g_recv.at[origin, h], dev)

    def chain_step(k):
        for h in range(2):
            for side, way, onward, behind in ways:
                origin = z - way * k
                here = (origin >= 0) & (origin < nz)
                if k > 0:
                    @pl.when(here)
                    def _():
                        chain(origin, -way, k, h).wait_recv()

                @pl.when(here & onward)
                def _():
                    chain(origin, way, k, h).start()

    for j in range(1, GROUP):
        w_copies[j].wait_recv()
    chain_step(0)

    def to_core(j):
        copy = remote(s_own.at[slot(j), :], s_sib.at[slot(j), :], c_send.at[j], c_recv.at[j], (me, sib))
        copy.start()
        core_copies.append(copy)

    relays = []
    for j, onto in ((1, 2), (2, 1)):
        s_copies[j].wait_recv()
        first = (j - 1) * (tok // 2)
        copy = remote(
            s_own.at[pl.ds(j * tok + first, tok // 2), :],
            s_own.at[pl.ds(3 * tok + first, tok // 2), :],
            s_send.at[2 + j], s_recv.at[2 + j], (me + steps[onto], core))
        copy.start()
        relays.append(copy)
    for i in range(1, nz):
        x_start(i)
    for j in (1, 2):
        to_core(j)
    chain_step(1)
    for copy in relays:
        copy.wait_recv()
    to_core(3)
    for copy in core_copies:
        copy.wait_recv()

    def partial_copy(t, side, lane, way):
        return remote(part_out.at[t, lane], part_in.at[side, t, lane],
                      p_send.at[t, lane], p_recv.at[side, t, lane], (me + GROUP * way, core))

    def toward(t, side):
        return t > z if side == 0 else t < z

    def block(i):
        t = order[i]
        for j in range(1, GROUP):
            x_copies[i, j].wait_recv()
        feature_rows = x_all[i]
        dims = (((0,), (0,)), ((), ()))
        for lane, grads in ((1, s_sib), (0, s_own)):
            part = lax.dot_general(feature_rows, grads[...], dims, preferred_element_type=jnp.float32)
            part_own[t, lane] = part
            for side, way, onward, behind in ways:
                @pl.when(toward(t, side) & jnp.logical_not(behind))
                def _():
                    part_out[t, lane] = part_own[t, lane].astype(jnp.bfloat16)
                    partial_copy(t, side, lane, way).start()

    def forward(i):
        t = order[i]
        for lane in (1, 0):
            for side, way, onward, behind in ways:
                @pl.when(toward(t, side) & behind)
                def _():
                    copy = partial_copy(t, side, lane, way)
                    copy.wait_recv()
                    part_out[t, lane] = (
                        part_own[t, lane] + part_in[side, t, lane].astype(jnp.float32)
                    ).astype(jnp.bfloat16)
                    copy.start()

    block(0)
    for k in range(2, nz):
        chain_step(k)
        if k == 2:
            block(1)

    o_copies = {}
    own_rows = pl.ds(pl.multiple_of(core * half, half), half)
    sib_rows = pl.ds(pl.multiple_of(sib * half, half), half)
    for j in (3, 1, 2, 0):
        product = jnp.dot(s_own[slot(j), :], w_all[own_rows, :], preferred_element_type=jnp.float32)
        product += jnp.dot(s_sib[slot(j), :], w_all[sib_rows, :], preferred_element_type=jnp.float32)
        if j == 0:
            dx_ref[:, lanes(quarter * fq, fq)] = product.astype(jnp.bfloat16)
        else:
            dx_out[j] = product.astype(jnp.bfloat16)
            o_copies[j] = remote(dx_out.at[j], dx_in.at[j], o_send.at[j], o_recv.at[j], (me + steps[j], core))
            o_copies[j].start()

    started = 2 if nz > 2 else 1
    for i in range(nz - started):
        block(i + started)
        forward(i)
    for i in range(nz - started, nz):
        forward(i)

    swap = remote(swap_out, swap_in, swap_send, swap_recv, (me, sib))
    mine = pl.ds(pl.multiple_of(core * hr, hr), hr)
    for lane in (1, 0):
        for side, way, onward, behind in ways:
            @pl.when(behind)
            def _():
                partial_copy(z, side, lane, -way).wait_recv()
                part_own[z, lane] = part_own[z, lane] + part_in[side, z, lane].astype(jnp.float32)
        total = part_own[z, lane] * normalizer
        if lane == 1:
            swap_out[...] = total
            swap.start()
        else:
            dw_ref[mine, :] = total

    for j in (1, 2, 3):
        o_copies[j].wait_recv()
        dx_ref[:, lanes((quarter + steps[j]) * fq, fq)] = dx_in[j]
    swap.wait_recv()
    dw_ref[pl.ds(pl.multiple_of(sib * hr, hr), hr), :] = swap_in[...]

    for group in (w_copies, s_copies, x_copies, o_copies):
        for copy in group.values():
            copy.wait_send()
    for copy in core_copies + relays + [swap]:
        copy.wait_send()
    for t in range(nz):
        for lane in range(2):
            for side, way, onward, behind in ways:
                @pl.when(toward(t, side))
                def _():
                    partial_copy(t, side, lane, way).wait_send()
    for k in range(nz):
        for h in range(2):
            for side, way, onward, behind in ways:
                origin = z - way * k

                @pl.when((origin >= 0) & (origin < nz) & onward)
                def _():
                    chain(origin, way, k, h).wait_send()


def fused(n, inputs, value_grad, value_weight, counts, offsets):
    tok, width = inputs.shape
    half = value_grad.shape[1]
    wfeat, wcols = value_weight.shape
    nz = n // GROUP
    fq = wfeat // GROUP
    hr = width // n // 2
    bf, f32, dma = jnp.bfloat16, jnp.float32, pltpu.SemaphoreType.DMA
    normalizer = 1.0 / math.sqrt(counts.shape[1] * n)
    vmem = pl.BlockSpec(memory_space=pltpu.VMEM)
    smem = pl.BlockSpec(memory_space=pltpu.SMEM)
    hbm = pl.BlockSpec(memory_space=pltpu.HBM)
    return pl.pallas_call(
        functools.partial(kernel, n, normalizer),
        out_shape=(
            jax.ShapeDtypeStruct((tok, wfeat), bf),
            jax.ShapeDtypeStruct((2 * hr, half), f32),
        ),
        in_specs=[smem] * 2 + [hbm] * 3,
        out_specs=(vmem, vmem),
        scratch_shapes=[
            pltpu.VMEM((tok, width), bf),
            pltpu.VMEM((tok, half), bf),
            pltpu.VMEM((wcols, wfeat), bf),
            pltpu.VMEM((tok, half), bf),
            pltpu.VMEM((GROUP * tok, half), bf),
            pltpu.VMEM((GROUP * tok, half), bf),
            pltpu.VMEM((nz, GROUP * tok, hr), bf),
            pltpu.VMEM((n * wcols, fq), bf),
            pltpu.VMEM((nz, 2, hr, half), f32),
            pltpu.VMEM((nz, 2, hr, half), bf),
            pltpu.VMEM((2, nz, 2, hr, half), bf),
            pltpu.VMEM((hr, half), f32),
            pltpu.VMEM((hr, half), f32),
            pltpu.VMEM((GROUP, tok, fq), bf),
            pltpu.VMEM((GROUP, tok, fq), bf),
            dma((3,)),
            dma((GROUP,)), dma((GROUP,)),
            dma((GROUP + 1,)), dma((GROUP + 1,)),
            dma((GROUP,)), dma((GROUP,)),
            dma((nz, GROUP)), dma((nz, GROUP)),
            dma((2, nz, 2)), dma((nz, 2)),
            dma((nz, 2)), dma((2, nz, 2)),
            dma((GROUP,)), dma((GROUP,)),
            dma, dma,
        ],
        compiler_params=pltpu.CompilerParams(
            collective_id=0, has_side_effects=True, vmem_limit_bytes=VMEM_ROOM
        ),
    )(counts, offsets, inputs, value_grad, value_weight.T)


def solution(mesh):
    n, tp = mesh.shape["fsdp"], mesh.shape["tp"]

    def local(inputs, value_grad, value_weight, counts, offsets):
        hr = inputs.shape[1] // n // 2
        fits = tp == 2 and n % GROUP == 0 and n > GROUP and hr % 128 == 0
        fits = fits and value_weight.shape[1] % 16 == 0
        if fits:
            return fused(n, inputs, value_grad, value_weight, counts, offsets)
        return general(inputs, value_grad, value_weight, counts, offsets)

    in_specs = (P("fsdp", None), P("fsdp", "tp"), P("tp", "fsdp"), P("fsdp", None), P("fsdp", None))
    out_specs = (P("fsdp", "tp"), P("fsdp", "tp"))
    return jax.shard_map(local, mesh=mesh, in_specs=in_specs, out_specs=out_specs, check_vma=False)
```

profile of v0, /device:TPU:0, one launch (start us, length us, event | category | flops | bytes accessed | tf_op | source)
XLA Modules:
  0.0 51.0 jit_solution(5397893373069408621)
XLA Ops:
  0.6 47.2 %shard_map.68 = (bf16[256,2048]{1,0:T(8,128)(2,1)}, f32[256,512]{1,0:T(8,128)}) custom-call(s32[1,4]{1,0:T(1,128)} %counts_ref.1, s32[1,4]{1,0:T(1,128)} %offsets_ref.1, bf16[256,4096]{1,0:T(8,128)(2,1)} %x_hbm.1, bf16[256,512]{1,0:T(8,128)(2,1)} %g_hbm.1, bf16[64,2048]{1,0:T(8,128)(2,1)} %bitcast.1), custom_call_target="tpu_custom_call" | custom-call | tf_op jit(solution)/shard_map/pallas_call | solution.py:338
  47.9 0.0 copy-start
  47.9 2.4 %copy.9 = bf16[256,2048]{1,0:T(8,128)(2,1)} copy(bf16[256,2048]{1,0:T(8,128)(2,1)} %get-tuple-element.4) | data formatting | bytes 2097152
  50.2 0.0 copy-done
  50.2 0.8 %copy.10 = f32[256,512]{1,0:T(8,128)} copy(f32[256,512]{1,0:T(8,128)S(1)} %copy-done) | data formatting | bytes 1048576
Async XLA Ops:
  47.9 2.4 %copy-start = (f32[256,512]{1,0:T(8,128)S(1)}, f32[256,512]{1,0:T(8,128)}, u32[]{:S(2)}) copy-start(f32[256,512]{1,0:T(8,128)} %get-tuple-element.5) | copy-start | bytes 1572868
where the time goes:
time: 51.2 us; the launch traced here: 51 us
  Pallas kernels  47.2 us (92%)
  local copies, waits for them, and re-layouts  3.16 us (6%)
  between operations  0.65 us (1%)
    pallas_call x1, Pallas kernels, fused(): pl.pallas_call(functools.partial(kernel, n, normalizer), out_shape=(jax.S...  47.2 us
    unnamed x4, local copies, waits for them, and re-layouts  3.16 us

commit v1 on v0

v1 whole, which is shorter than its diff:
```python
import functools
import math

import jax
import jax.numpy as jnp
from jax import lax
from jax.experimental import pallas as pl
from jax.experimental.pallas import tpu as pltpu
from jax.sharding import PartitionSpec as P

MESH = pl.DeviceIdType.MESH
GROUP = 4
VMEM_ROOM = 54 * 2**20


def scale_rows(value_grad, counts, offsets):
    positions = jnp.arange(value_grad.shape[0], dtype=jnp.int32)[:, None]
    starts = offsets[0][None, :]
    lengths = counts[0][None, :]
    inside = (positions >= starts) & (positions < starts + lengths)
    inverse_root = lax.rsqrt(lengths.astype(jnp.float32))
    row_factor = jnp.sum(jnp.where(inside, inverse_root, jnp.zeros_like(inverse_root)), axis=1)
    return (value_grad.astype(jnp.float32) * row_factor[:, None]).astype(jnp.bfloat16)


def general(inputs, value_grad, value_weight, counts, offsets):
    tok_rows = inputs.shape[0]
    row_block = min(128, tok_rows)
    scaled = scale_rows(value_grad, counts, offsets)
    live_end = jnp.max(offsets[0] + counts[0])
    live_blocks = (live_end + row_block - 1) // row_block
    scaled_all = lax.all_gather(scaled, "tp", axis=1, tiled=True)
    empty_inputs = jnp.zeros((tok_rows, value_weight.shape[0]), jnp.float32)
    piece = lax.all_gather(value_weight, "fsdp", axis=1, tiled=True)

    def add_add_block(block_index, partial_value):
        lower = lax.dynamic_slice_in_dim(scaled_all, block_index * row_block, row_block, 0)
        before = lax.dynamic_slice_in_dim(partial_value, block_index * row_block, row_block, 0)
        product = lax.dot_general(
            lower, piece, (((1,), (1,)), ((), ())), preferred_element_type=jnp.float32
        )
        return lax.dynamic_update_slice_in_dim(
            partial_value, before + product, block_index * row_block, 0
        )

    result = lax.fori_loop(0, live_blocks, add_add_block, empty_inputs)
    input_grad = result.astype(jnp.bfloat16)
    normalizer = 1.0 / math.sqrt(counts.shape[1] * lax.axis_size("fsdp"))
    empty = jnp.zeros((inputs.shape[1], scaled.shape[1]), jnp.float32)

    def weight_add_block(block_index, partial_value):
        feature_rows = lax.dynamic_slice_in_dim(inputs, block_index * row_block, row_block, 0)
        grad_rows = lax.dynamic_slice_in_dim(scaled, block_index * row_block, row_block, 0)
        return partial_value + lax.dot_general(
            feature_rows, grad_rows, (((0,), (0,)), ((), ())), preferred_element_type=jnp.float32
        )

    result = lax.fori_loop(0, live_blocks, weight_add_block, empty)
    summed = lax.psum_scatter(result, "fsdp", scatter_dimension=0, tiled=True)
    return (input_grad, summed * normalizer)


def kernel(
    n, normalizer, counts_ref, offsets_ref, x_hbm, g_hbm, wt_hbm, dx_ref, dw_ref,
    g_ref, wt_ref, x_src, s_all, x_all, w_all, acc, part_own, part_out, part_in, dx_out,
    local_sem, xf_sem, xo_sem, w_send, w_recv, s_send, s_recv, c_send, c_recv, x_send, x_recv,
    xs_send, xs_recv, g_send, g_recv, p_send, p_recv, o_send, o_recv,
):
    nz = n // GROUP
    me = lax.axis_index("fsdp")
    core = lax.axis_index("tp")
    sib = 1 - core
    z = me // GROUP
    quarter = me % GROUP
    dx = 1 - 2 * (me % 2)
    dy = 2 - 4 * ((me // 2) % 2)
    steps = (0, dx, dy, dx + dy)
    tok, half = g_ref.shape
    wcols = wt_ref.shape[0]
    fq = w_all.shape[1]
    hr = x_src.shape[3]
    upper = (2 * z) // nz
    order = [a + upper * (nz - 1 - 2 * a) for a in
             list(range(nz - 1, nz // 2 - 1, -1)) + list(range(nz // 2))]

    def remote(src, dst, send, recv, dev):
        return pltpu.make_async_remote_copy(
            src_ref=src, dst_ref=dst, send_sem=send, recv_sem=recv,
            device_id=dev, device_id_type=MESH,
        )

    def w_rows(f):
        return pl.ds(pl.multiple_of(f * wcols, wcols), wcols)

    def lanes(start, size):
        return pl.ds(pl.multiple_of(start, 128), size)

    def slot(j):
        return pl.ds(j * tok, tok)

    def x_lanes(i, q, h):
        return lanes(((order[i] * GROUP + q) * 2 + h) * hr, hr)

    fetch_w = pltpu.make_async_copy(wt_hbm, wt_ref, local_sem.at[0])
    fetch_own = pltpu.make_async_copy(
        wt_hbm.at[:, lanes(quarter * fq, fq)], w_all.at[w_rows(me), :], local_sem.at[1])
    fetch_g = pltpu.make_async_copy(g_hbm, g_ref, local_sem.at[2])
    for fetch in (fetch_w, fetch_own, fetch_g):
        fetch.start()

    barrier = pltpu.get_barrier_semaphore()
    for j in range(1, GROUP):
        pl.semaphore_signal(barrier, inc=1, device_id=(me + steps[j], core), device_id_type=MESH)
    pl.semaphore_signal(barrier, inc=1, device_id=(me, sib), device_id_type=MESH)
    ways = ((0, 1, z < nz - 1, z > 0), (1, -1, z > 0, z < nz - 1))
    for side, way, onward, behind in ways:
        @pl.when(onward)
        def _():
            pl.semaphore_signal(barrier, inc=1, device_id=(me + GROUP * way, core), device_id_type=MESH)

    x_fetches, own_fetches = {}, {}
    for i in range(nz):
        for j in (3, 1, 2):
            x_fetches[i, j] = pltpu.make_async_copy(
                x_hbm.at[:, x_lanes(i, quarter + steps[j], core)], x_src.at[i, j - 1], xf_sem.at[i, j - 1])
            x_fetches[i, j].start()
        for h in range(2):
            own_fetches[i, h] = pltpu.make_async_copy(
                x_hbm.at[:, x_lanes(i, quarter, h)], x_all.at[i, h, slot(0), :], xo_sem.at[i, h])
            own_fetches[i, h].start()

    fetch_w.wait()
    fetch_own.wait()
    inner = (z > 0) & (z < nz - 1)

    @pl.when(inner)
    def _():
        pl.semaphore_wait(barrier, GROUP + 2)

    @pl.when(jnp.logical_not(inner))
    def _():
        pl.semaphore_wait(barrier, GROUP + 1)

    w_copies, s_copies, x_copies, core_copies = {}, {}, {}, {}
    for j in (3, 1, 2):
        w_copies[j] = remote(
            wt_ref.at[:, lanes((quarter + steps[j]) * fq, fq)], w_all.at[w_rows(me), :],
            w_send.at[j], w_recv.at[j], (me + steps[j], core))
        w_copies[j].start()

    def chain(origin, way, k, j):
        rows = w_rows(origin * GROUP + quarter + steps[j])
        dev = (me + GROUP * way, core)
        return remote(w_all.at[rows, :], w_all.at[rows, :],
                      g_send.at[(1 - way) // 2, k, j], g_recv.at[origin, j], dev)

    def chain_pass(k, j):
        for side, way, onward, behind in ways:
            origin = z - way * k

            @pl.when((origin >= 0) & (origin < nz) & onward)
            def _():
                if k > 0:
                    chain(origin, -way, k, j).wait_recv()
                chain(origin, way, k, j).start()

    def chain_end(k):
        for side, way, onward, behind in ways:
            origin = z - way * k

            @pl.when((origin >= 0) & (origin < nz) & jnp.logical_not(onward))
            def _():
                for j in range(GROUP):
                    chain(origin, -way, k, j).wait_recv()

    chain_pass(0, 0)

    fetch_g.wait()
    positions = lax.broadcasted_iota(jnp.int32, (tok, 128), 0)
    factor = jnp.zeros((tok, 128), jnp.float32)
    for i in range(counts_ref.shape[1]):
        start = jnp.full((tok, 128), offsets_ref[0, i], jnp.int32)
        length = jnp.full((tok, 128), counts_ref[0, i], jnp.int32)
        inside = (positions >= start) & (positions < start + length)
        factor += jnp.where(inside, lax.rsqrt(length.astype(jnp.float32)), 0.0)
    for i in range(half // 128):
        cols = slice(i * 128, (i + 1) * 128)
        s_all[core, 0:tok, cols] = (g_ref[:, cols].astype(jnp.float32) * factor).astype(jnp.bfloat16)

    hop = tok // 2

    def s_rows(j, h):
        return ((j - 1 + h) % 2) * hop

    for h in range(2):
        for j in (1, 2):
            s_copies[j, h] = remote(
                s_all.at[core, pl.ds(s_rows(j, h), hop), :],
                s_all.at[core, pl.ds(j * tok + s_rows(j, h), hop), :],
                s_send.at[2 * j - 2 + h], s_recv.at[2 * j - 2 + h], (me + steps[j], core))
            s_copies[j, h].start()

    def to_core(j):
        core_copies[j] = remote(
            s_all.at[core, slot(j), :], s_all.at[core, slot(j), :], c_send.at[j], c_recv.at[j], (me, sib))
        core_copies[j].start()

    to_core(0)
    for j in (2, 3, 1):
        w_copies[j].wait_recv()
        chain_pass(0, j)

    for j, onto in ((1, 2), (2, 1)):
        s_copies[j, 0].wait_recv()
        s_copies[3, j - 1] = remote(
            s_all.at[core, pl.ds(j * tok + s_rows(j, 0), hop), :],
            s_all.at[core, pl.ds(3 * tok + s_rows(j, 0), hop), :],
            s_send.at[3 + j], s_recv.at[3 + j], (me + steps[onto], core))
        s_copies[3, j - 1].start()

    for i in range(nz):
        for j in (3, 1, 2):
            x_fetches[i, j].wait()
            x_copies[i, j] = remote(
                x_src.at[i, j - 1], x_all.at[i, core, slot(j), :],
                x_send.at[i, j], x_recv.at[i, j], (me + steps[j], core))
            x_copies[i, j].start()

    for j in (0, 2, 3, 1):
        chain_pass(1, j)
    for j in (1, 2):
        s_copies[j, 1].wait_recv()
        to_core(j)
    for h in range(2):
        s_copies[3, h].wait_recv()
    to_core(3)
    chain_end(1)
    for j in range(GROUP):
        core_copies[j].wait_recv()
    near = pl.ds(pl.multiple_of(upper * half, half), half)
    far = pl.ds(pl.multiple_of((1 - upper) * half, half), half)
    for j in range(GROUP):
        acc[slot(j), :] = jnp.dot(s_all[upper, slot(j), :], w_all[near, :], preferred_element_type=jnp.float32)
    for k in range(2, nz):
        for j in (0, 2, 3, 1):
            chain_pass(k, j)

    def partial_copy(t, side, h, way):
        return remote(part_out.at[t, h], part_in.at[side, t, h],
                      p_send.at[t, h], p_recv.at[side, t, h], (me + GROUP * way, core))

    def toward(t, side):
        return t > z if side == 0 else t < z

    xs_copies = {}

    def block(i):
        t = order[i]
        for j in range(1, GROUP):
            x_copies[i, j].wait_recv()
        arrived = x_all.at[i, core, pl.ds(tok, (GROUP - 1) * tok), :]
        xs_copies[i] = remote(arrived, arrived, xs_send.at[i], xs_recv.at[i], (me, sib))
        xs_copies[i].start()
        for h in range(2):
            own_fetches[i, h].wait()
        for h in (core, sib):
            if h is sib:
                xs_copies[i].wait_recv()
            part_own[t, h] = lax.dot_general(
                x_all[i, h], s_all[core], (((0,), (0,)), ((), ())), preferred_element_type=jnp.float32)
            for side, way, onward, behind in ways:
                @pl.when(toward(t, side) & jnp.logical_not(behind))
                def _():
                    part_out[t, h] = part_own[t, h].astype(jnp.bfloat16)
                    partial_copy(t, side, h, way).start()

    def forward(i, h):
        t = order[i]
        for side, way, onward, behind in ways:
            @pl.when(toward(t, side) & behind)
            def _():
                copy = partial_copy(t, side, h, way)
                copy.wait_recv()
                part_out[t, h] = (
                    part_own[t, h] + part_in[side, t, h].astype(jnp.float32)
                ).astype(jnp.bfloat16)
                copy.start()

    block(0)
    block(1)
    for k in range(2, nz):
        chain_end(k)
    o_copies = {}
    own_lanes = lanes(quarter * fq, fq)
    for j in (3, 1, 2, 0):
        product = acc[slot(j), :] + jnp.dot(
            s_all[1 - upper, slot(j), :], w_all[far, :], preferred_element_type=jnp.float32)
        if j == 0:
            dx_ref[:, own_lanes] = product.astype(jnp.bfloat16)
        else:
            dx_out[j] = product.astype(jnp.bfloat16)
            o_copies[j] = remote(
                dx_out.at[j], dx_ref.at[:, own_lanes], o_send.at[j], o_recv.at[j], (me + steps[j], core))
            o_copies[j].start()

    for h in (core, sib):
        forward(0, h)
    for i in range(2, nz):
        block(i)
    for h in (core, sib):
        for i in list(range(2, nz)) + [1]:
            forward(i, h)

    for h in (core, sib):
        for side, way, onward, behind in ways:
            @pl.when(behind)
            def _():
                partial_copy(z, side, h, -way).wait_recv()
                part_own[z, h] = part_own[z, h] + part_in[side, z, h].astype(jnp.float32)
        dw_ref[pl.ds(pl.multiple_of(h * hr, hr), hr), :] = part_own[z, h] * normalizer

    for j in (1, 2, 3):
        remote(dx_out.at[j], dx_ref.at[:, lanes((quarter + steps[j]) * fq, fq)],
               o_send.at[j], o_recv.at[j], (me + steps[j], core)).wait_recv()

    for group in (w_copies, s_copies, x_copies, o_copies, core_copies, xs_copies):
        for copy in group.values():
            copy.wait_send()
    for t in range(nz):
        for h in range(2):
            for side, way, onward, behind in ways:
                @pl.when(toward(t, side))
                def _():
                    partial_copy(t, side, h, way).wait_send()
    for k in range(nz):
        for j in range(GROUP):
            for side, way, onward, behind in ways:
                origin = z - way * k

                @pl.when((origin >= 0) & (origin < nz) & onward)
                def _():
                    chain(origin, way, k, j).wait_send()


def emit(dx_ref, dw_ref, dx_out, dw_out, sems):
    copies = [
        pltpu.make_async_copy(dx_ref, dx_out, sems.at[0]),
        pltpu.make_async_copy(dw_ref, dw_out, sems.at[1]),
    ]
    for copy in copies:
        copy.start()
    for copy in copies:
        copy.wait()


def fused(n, inputs, value_grad, value_weight, counts, offsets):
    tok, width = inputs.shape
    half = value_grad.shape[1]
    wfeat, wcols = value_weight.shape
    nz = n // GROUP
    fq = wfeat // GROUP
    hr = width // n // 2
    bf, f32, dma = jnp.bfloat16, jnp.float32, pltpu.SemaphoreType.DMA
    normalizer = 1.0 / math.sqrt(counts.shape[1] * n)
    vmem = pl.BlockSpec(memory_space=pltpu.VMEM)
    smem = pl.BlockSpec(memory_space=pltpu.SMEM)
    hbm = pl.BlockSpec(memory_space=pltpu.HBM)
    held = pl.pallas_call(
        functools.partial(kernel, n, normalizer),
        out_shape=(pltpu.VMEM((tok, wfeat), bf), pltpu.VMEM((2 * hr, half), f32)),
        in_specs=[smem] * 2 + [hbm] * 3,
        out_specs=(vmem, vmem),
        scratch_shapes=[
            pltpu.VMEM((tok, half), bf),
            pltpu.VMEM((wcols, wfeat), bf),
            pltpu.VMEM((nz, GROUP - 1, tok, hr), bf),
            pltpu.VMEM((2, GROUP * tok, half), bf),
            pltpu.VMEM((nz, 2, GROUP * tok, hr), bf),
            pltpu.VMEM((n * wcols, fq), bf),
            pltpu.VMEM((GROUP * tok, fq), f32),
            pltpu.VMEM((nz, 2, hr, half), f32),
            pltpu.VMEM((nz, 2, hr, half), bf),
            pltpu.VMEM((2, nz, 2, hr, half), bf),
            pltpu.VMEM((GROUP, tok, fq), bf),
            dma((3,)), dma((nz, GROUP - 1)), dma((nz, 2)),
            dma((GROUP,)), dma((GROUP,)),
            dma((6,)), dma((6,)),
            dma((GROUP,)), dma((GROUP,)),
            dma((nz, GROUP)), dma((nz, GROUP)),
            dma((nz,)), dma((nz,)),
            dma((2, nz, GROUP)), dma((nz, GROUP)),
            dma((nz, 2)), dma((2, nz, 2)),
            dma((GROUP,)), dma((GROUP,)),
        ],
        compiler_params=pltpu.CompilerParams(
            collective_id=0, has_side_effects=True, vmem_limit_bytes=VMEM_ROOM
        ),
    )(counts, offsets, inputs, value_grad, value_weight.T)
    return pl.pallas_call(
        emit,
        out_shape=(
            jax.ShapeDtypeStruct((tok, wfeat), bf),
            jax.ShapeDtypeStruct((2 * hr, half), f32),
        ),
        in_specs=[vmem] * 2,
        out_specs=(hbm, hbm),
        scratch_shapes=[dma((2,))],
    )(*[pltpu.with_memory_space_constraint(part, pltpu.VMEM) for part in held])


def solution(mesh):
    n, tp = mesh.shape["fsdp"], mesh.shape["tp"]

    def local(inputs, value_grad, value_weight, counts, offsets):
        hr = inputs.shape[1] // n // 2
        fits = tp == 2 and n % (2 * GROUP) == 0 and n > 2 * GROUP and hr % 128 == 0
        fits = fits and value_weight.shape[1] % 16 == 0 and inputs.shape[0] % 32 == 0
        if fits:
            return fused(n, inputs, value_grad, value_weight, counts, offsets)
        return general(inputs, value_grad, value_weight, counts, offsets)

    in_specs = (P("fsdp", None), P("fsdp", "tp"), P("tp", "fsdp"), P("fsdp", None), P("fsdp", None))
    out_specs = (P("fsdp", "tp"), P("fsdp", "tp"))
    return jax.shard_map(local, mesh=mesh, in_specs=in_specs, out_specs=out_specs, check_vma=False)
```

time: 51.2 us -> 45.3 us (0.88)
  local copies, waits for them, and re-layouts: 3.16 us -> 0 us
  Pallas kernels: 47.2 us -> 44.5 us
    unnamed x4 -> x0, local copies, waits for them, and re-layouts: 3.16 us -> none
    pallas_call x1 -> x2, Pallas kernels: 47.2 us -> 44.5 us  [the longest x1 43.3 us: fused(): pl.pallas_call(functools.partial(kernel, n, normalizer), out_shape=(pltpu...]
where the time goes in v1:
time: 45.3 us; the launch traced here: 45.1 us
  Pallas kernels  44.5 us (98%)
  between operations  0.64 us (1%)
    pallas_call x1, Pallas kernels, fused(): pl.pallas_call(functools.partial(kernel, n, normalizer), out_shape=(pltpu...  43.3 us
    pallas_call x1, Pallas kernels, fused(): pl.pallas_call(emit, out_shape=(jax.ShapeDtypeStruct((tok, wfeat), bf), j...  1.16 us

profile of v1, /device:TPU:0, one launch (start us, length us, event | category | flops | bytes accessed | tf_op | source)
XLA Modules:
  0.0 45.1 jit_solution(15707889077561488299)
XLA Ops:
  0.6 43.3 %shard_map.68 = (bf16[256,2048]{1,0:T(8,128)(2,1)S(1)}, f32[256,512]{1,0:T(8,128)S(1)}) custom-call(s32[1,4]{1,0:T(1,128)} %counts_ref.1, s32[1,4]{1,0:T(1,128)} %offsets_ref.1, bf16[256,4096]{1,0:T(8,128)(2,1)} %x_hbm.1, bf16[256,512]{1,0:T(8,128)(2,1)} %g_hbm.1, bf16[64,2048]{1,0:T(8,128)(2,1)} %bitcast.1), custom_call_target="tpu_custom_call" | custom-call | tf_op jit(solution)/shard_map/pallas_call | solution.py:368
  43.9 1.2 %shard_map.69 = (bf16[256,2048]{1,0:T(8,128)(2,1)}, f32[256,512]{1,0:T(8,128)}) custom-call(bf16[256,2048]{1,0:T(8,128)(2,1)S(1)} %get-tuple-element.4.dx_ref, f32[256,512]{1,0:T(8,128)S(1)} %get-tuple-element.5.dw_ref), custom_call_target="tpu_custom_call" | custom-call | tf_op jit(solution)/shard_map/pallas_call | solution.py:399

commit v2 on v1

v2 whole, which is shorter than its diff:
```python
import functools
import math

import jax
import jax.numpy as jnp
from jax import lax
from jax.experimental import pallas as pl
from jax.experimental.pallas import tpu as pltpu
from jax.sharding import PartitionSpec as P

MESH = pl.DeviceIdType.MESH
GROUP = 4
LANES = 4
VMEM_ROOM = 54 * 2**20


def scale_rows(value_grad, counts, offsets):
    positions = jnp.arange(value_grad.shape[0], dtype=jnp.int32)[:, None]
    starts = offsets[0][None, :]
    lengths = counts[0][None, :]
    inside = (positions >= starts) & (positions < starts + lengths)
    inverse_root = lax.rsqrt(lengths.astype(jnp.float32))
    row_factor = jnp.sum(jnp.where(inside, inverse_root, jnp.zeros_like(inverse_root)), axis=1)
    return (value_grad.astype(jnp.float32) * row_factor[:, None]).astype(jnp.bfloat16)


def general(inputs, value_grad, value_weight, counts, offsets):
    tok_rows = inputs.shape[0]
    row_block = min(128, tok_rows)
    scaled = scale_rows(value_grad, counts, offsets)
    live_end = jnp.max(offsets[0] + counts[0])
    live_blocks = (live_end + row_block - 1) // row_block
    scaled_all = lax.all_gather(scaled, "tp", axis=1, tiled=True)
    empty_inputs = jnp.zeros((tok_rows, value_weight.shape[0]), jnp.float32)
    piece = lax.all_gather(value_weight, "fsdp", axis=1, tiled=True)

    def add_add_block(block_index, partial_value):
        lower = lax.dynamic_slice_in_dim(scaled_all, block_index * row_block, row_block, 0)
        before = lax.dynamic_slice_in_dim(partial_value, block_index * row_block, row_block, 0)
        product = lax.dot_general(
            lower, piece, (((1,), (1,)), ((), ())), preferred_element_type=jnp.float32
        )
        return lax.dynamic_update_slice_in_dim(
            partial_value, before + product, block_index * row_block, 0
        )

    result = lax.fori_loop(0, live_blocks, add_add_block, empty_inputs)
    input_grad = result.astype(jnp.bfloat16)
    normalizer = 1.0 / math.sqrt(counts.shape[1] * lax.axis_size("fsdp"))
    empty = jnp.zeros((inputs.shape[1], scaled.shape[1]), jnp.float32)

    def weight_add_block(block_index, partial_value):
        feature_rows = lax.dynamic_slice_in_dim(inputs, block_index * row_block, row_block, 0)
        grad_rows = lax.dynamic_slice_in_dim(scaled, block_index * row_block, row_block, 0)
        return partial_value + lax.dot_general(
            feature_rows, grad_rows, (((0,), (0,)), ((), ())), preferred_element_type=jnp.float32
        )

    result = lax.fori_loop(0, live_blocks, weight_add_block, empty)
    summed = lax.psum_scatter(result, "fsdp", scatter_dimension=0, tiled=True)
    return (input_grad, summed * normalizer)


def kernel(
    n, normalizer, counts_hbm, offsets_hbm, x_hbm, g_hbm, wt_hbm, dx_ref, dw_ref,
    counts_ref, offsets_ref, g_ref, wt_ref, x_src, s_all, x_all, w_all, acc, part_own, part_out, part_in,
    dx_out, local_sem, w_send, w_recv, s_send, s_recv, c_send, c_recv, x_send, x_recv,
    xs_send, xs_recv, g_send, g_recv, p_send, p_recv, o_send, o_recv,
):
    nz = n // GROUP
    me = lax.axis_index("fsdp")
    core = lax.axis_index("tp")
    sib = 1 - core
    z = me // GROUP
    quarter = me % GROUP
    dx = 1 - 2 * (me % 2)
    dy = 2 - 4 * ((me // 2) % 2)
    steps = (0, dx, dy, dx + dy)
    tok, half = g_ref.shape
    wcols = wt_ref.shape[0]
    fq = w_all.shape[1]
    hr = x_src.shape[3]
    zrows = GROUP * wcols
    lane_rows = part_out.shape[1] // LANES
    upper = (2 * z) // nz
    order = [a + upper * (nz - 1 - 2 * a) for a in
             list(range(nz - 1, nz // 2 - 1, -1)) + list(range(nz // 2))]
    ways = ((0, 1, z < nz - 1, z > 0), (1, -1, z > 0, z < nz - 1))
    inner = (z > 0) & (z < nz - 1)

    barrier = pltpu.get_barrier_semaphore()
    for j in range(1, GROUP):
        pl.semaphore_signal(barrier, inc=1, device_id=(me + steps[j], core), device_id_type=MESH)
    pl.semaphore_signal(barrier, inc=1, device_id=(me, sib), device_id_type=MESH)
    for side, way, onward, behind in ways:
        @pl.when(onward)
        def _():
            pl.semaphore_signal(barrier, inc=1, device_id=(me + GROUP * way, core), device_id_type=MESH)

    def remote(src, dst, send, recv, dev):
        return pltpu.make_async_remote_copy(
            src_ref=src, dst_ref=dst, send_sem=send, recv_sem=recv,
            device_id=dev, device_id_type=MESH,
        )

    def sent(ref, sem):
        remote(ref, ref, sem, sem, (me, sib)).wait_send()

    def received(ref, sem):
        remote(ref, ref, sem, sem, (me, sib)).wait_recv()

    def w_rows(f):
        return pl.ds(pl.multiple_of(f * wcols, wcols), wcols)

    def lanes(start, size):
        return pl.ds(pl.multiple_of(start, 128), size)

    def slot(j):
        return pl.ds(j * tok, tok)

    def x_lanes(i, q, h):
        return lanes(((order[i] * GROUP + q) * 2 + h) * hr, hr)

    others = pl.ds(tok, (GROUP - 1) * tok)
    mine = lanes(core * hr, hr)

    fetch_w = pltpu.make_async_copy(wt_hbm, wt_ref, local_sem.at[0])
    fetch_own = pltpu.make_async_copy(
        wt_hbm.at[:, lanes(quarter * fq, fq)], w_all.at[w_rows(me), :], local_sem.at[1])
    fetch_g = pltpu.make_async_copy(g_hbm, g_ref, local_sem.at[2])
    fetch_counts = pltpu.make_async_copy(counts_hbm, counts_ref, local_sem.at[3])
    fetch_offsets = pltpu.make_async_copy(offsets_hbm, offsets_ref, local_sem.at[4])
    for fetch in (fetch_w, fetch_own, fetch_g, fetch_counts, fetch_offsets):
        fetch.start()
    for i in range(nz):
        for j in (3, 1, 2):
            pltpu.make_async_copy(
                x_hbm.at[:, x_lanes(i, quarter + steps[j], core)], x_src.at[i, j - 1], local_sem.at[5]).start()
    for i in range(nz):
        block_lanes = lanes((order[i] * GROUP + quarter) * 2 * hr, 2 * hr)
        pltpu.make_async_copy(x_hbm.at[:, block_lanes], x_all.at[i, slot(0), :], local_sem.at[6]).start()

    fetch_w.wait()
    fetch_own.wait()

    @pl.when(inner)
    def _():
        pl.semaphore_wait(barrier, GROUP + 2)

    @pl.when(jnp.logical_not(inner))
    def _():
        pl.semaphore_wait(barrier, GROUP + 1)

    for j in (3, 1, 2):
        remote(wt_ref.at[:, lanes((quarter + steps[j]) * fq, fq)], w_all.at[w_rows(me), :],
               w_send, w_recv.at[j - 1], (me + steps[j], core)).start()

    def chain(origin, way, j):
        rows = w_rows(origin * GROUP + quarter + steps[j])
        return remote(w_all.at[rows, :], w_all.at[rows, :],
                      g_send.at[(1 - way) // 2], g_recv.at[origin, j], (me + GROUP * way, core))

    def chain_pass(k, j):
        for side, way, onward, behind in ways:
            origin = z - way * k

            @pl.when((origin >= 0) & (origin < nz) & onward)
            def _():
                if k > 0:
                    chain(origin, -way, j).wait_recv()
                chain(origin, way, j).start()

    def chain_end(k):
        for side, way, onward, behind in ways:
            origin = z - way * k

            @pl.when((origin >= 0) & (origin < nz) & jnp.logical_not(onward))
            def _():
                for j in range(GROUP):
                    chain(origin, -way, j).wait_recv()

    chain_pass(0, 0)

    for fetch in (fetch_g, fetch_counts, fetch_offsets):
        fetch.wait()
    positions = lax.broadcasted_iota(jnp.int32, (tok, 128), 0)
    factor = jnp.zeros((tok, 128), jnp.float32)
    for i in range(counts_ref.shape[1]):
        start = jnp.full((tok, 128), offsets_ref[0, i], jnp.int32)
        length = jnp.full((tok, 128), counts_ref[0, i], jnp.int32)
        inside = (positions >= start) & (positions < start + length)
        factor += jnp.where(inside, lax.rsqrt(length.astype(jnp.float32)), 0.0)
    for i in range(half // 128):
        cols = slice(i * 128, (i + 1) * 128)
        s_all[core, 0:tok, cols] = (g_ref[:, cols].astype(jnp.float32) * factor).astype(jnp.bfloat16)

    hop = tok // 2

    def s_send_rows(j, src_slot, dst_slot, h, sem, onto):
        first = ((j - 1 + h) % 2) * hop
        remote(s_all.at[core, pl.ds(src_slot * tok + first, hop), :],
               s_all.at[core, pl.ds(dst_slot * tok + first, hop), :],
               s_send, s_recv.at[sem], (me + steps[onto], core)).start()

    for h in range(2):
        for j in (1, 2):
            s_send_rows(j, 0, j, h, 2 if h else j - 1, j)

    def to_core(first, count):
        rows = pl.ds(first * tok, count * tok)
        remote(s_all.at[core, rows, :], s_all.at[core, rows, :], c_send, c_recv, (me, sib)).start()

    to_core(0, 1)

    def x_start(i):
        for j in (3, 1, 2):
            remote(x_src.at[i, j - 1], x_all.at[i, slot(j), mine],
                   x_send, x_recv.at[i], (me + steps[j], core)).start()

    pltpu.make_async_copy(x_src, x_src, local_sem.at[5]).wait()
    x_start(0)
    for j in (2, 3, 1):
        received(w_all.at[w_rows(me), :], w_recv.at[j - 1])
        chain_pass(0, j)
    for j, onto in ((1, 2), (2, 1)):
        received(s_all.at[core, pl.ds(0, hop), :], s_recv.at[j - 1])
        s_send_rows(j, j, 3, 0, 3, onto)
    for i in range(1, nz):
        x_start(i)
    for j in (0, 2, 3, 1):
        chain_pass(1, j)
    received(s_all.at[core, pl.ds(0, 2 * hop), :], s_recv.at[2])
    to_core(1, 2)

    def partial_copy(t, side, lane, way, target):
        place = t if side == 0 else jnp.where(t == target, nz, t)
        rows = pl.ds(lane * lane_rows, lane_rows)
        return remote(part_out.at[t, rows, :], part_in.at[place, rows, :],
                      p_send, p_recv.at[place, lane], (me + GROUP * way, core))

    def toward(t, side):
        return t > z if side == 0 else t < z

    def x_swap(i):
        received(x_all.at[i, others, mine], x_recv.at[i])
        remote(x_all.at[i, others, mine], x_all.at[i, others, mine], xs_send, xs_recv.at[i], (me, sib)).start()

    def contract(i, rows):
        return lax.dot_general(x_all[i, rows, :], s_all[core, rows, :], (((0,), (0,)), ((), ())),
                               preferred_element_type=jnp.float32)

    def launch(i):
        t = order[i]
        for side, way, onward, behind in ways:
            @pl.when(toward(t, side) & jnp.logical_not(behind))
            def _():
                for lane in range(LANES):
                    rows = pl.ds(lane * lane_rows, lane_rows)
                    part_out[t, rows, :] = part_own[t, rows, :].astype(jnp.bfloat16)
                    partial_copy(t, side, lane, way, z + way).start()

    def block(i):
        x_swap(i)
        received(x_all.at[i, others, mine], xs_recv.at[i])
        part_own[order[i]] = contract(i, pl.ds(0, GROUP * tok))
        launch(i)

    def forward(i, lane):
        t = order[i]
        rows = pl.ds(lane * lane_rows, lane_rows)
        for side, way, onward, behind in ways:
            @pl.when(toward(t, side) & behind)
            def _():
                partial_copy(t, side, lane, -way, z).wait_recv()
                part_out[t, rows, :] = (
                    part_own[t, rows, :] + part_in[t, rows, :].astype(jnp.float32)
                ).astype(jnp.bfloat16)
                partial_copy(t, side, lane, way, z + way).start()

    pltpu.make_async_copy(x_all.at[:, slot(0), :], x_all.at[:, slot(0), :], local_sem.at[6]).wait()
    x_swap(0)
    received(x_all.at[0, others, mine], xs_recv.at[0])
    part_own[order[0]] = contract(0, pl.ds(0, (GROUP - 1) * tok))
    for k in range(2, nz):
        for j in (0, 2, 3, 1):
            chain_pass(k, j)
    received(s_all.at[core, pl.ds(0, 2 * hop), :], s_recv.at[3])
    to_core(3, 1)
    part_own[order[0]] = part_own[order[0]] + contract(0, slot(GROUP - 1))
    launch(0)

    chain_end(1)
    received(s_all.at[core], c_recv)
    near = pl.ds(pl.multiple_of(upper * half, half), half)
    far = pl.ds(pl.multiple_of((1 - upper) * half, half), half)
    for j in range(GROUP):
        acc[slot(j), :] = jnp.dot(s_all[upper, slot(j), :], w_all[near, :], preferred_element_type=jnp.float32)
    block(1)
    for k in range(2, nz):
        chain_end(k)
    own_lanes = lanes(quarter * fq, fq)
    first = jnp.where(quarter == 1, 1, GROUP - 1)
    for j, step in ((first, jnp.where(quarter == 1, steps[1], steps[3])),
                    (GROUP - first, jnp.where(quarter == 1, steps[3], steps[1])),
                    (2, steps[2]), (0, None)):
        rows = pl.ds(pl.multiple_of(j * tok, tok), tok)
        product = acc[rows, :] + jnp.dot(
            s_all[1 - upper, rows, :], w_all[far, :], preferred_element_type=jnp.float32)
        if step is None:
            dx_ref[:, own_lanes] = product.astype(jnp.bfloat16)
        else:
            dx_out[j - 1] = product.astype(jnp.bfloat16)
            remote(dx_out.at[j - 1], dx_ref.at[:, own_lanes], o_send, o_recv, (me + step, core)).start()

    for lane in range(LANES):
        forward(0, lane)
    for i in range(2, nz):
        block(i)
    for lane in range(LANES):
        for i in list(range(2, nz)) + [1]:
            forward(i, lane)

    for lane in range(LANES):
        rows = pl.ds(lane * lane_rows, lane_rows)
        for side, way, onward, behind in ways:
            @pl.when(behind)
            def _():
                partial_copy(z, side, lane, -way, z).wait_recv()
                place = z if side == 0 else nz
                part_own[z, rows, :] = part_own[z, rows, :] + part_in[place, rows, :].astype(jnp.float32)
        dw_ref[rows, :] = part_own[z, rows, :] * normalizer

    received(dx_out, o_recv)

    sent(w_all.at[pl.ds(0, (GROUP - 1) * wcols), :], w_send)
    sent(s_all.at[0, others, :], s_send)
    sent(s_all.at[0], c_send)
    sent(x_src, x_send)
    sent(x_all.at[:, others, mine], xs_send)
    sent(dx_out, o_send)
    sent(part_out.at[pl.ds(0, nz - 1)], p_send)
    for level in range(nz):
        @pl.when(z == level)
        def _():
            if level < nz - 1:
                sent(w_all.at[pl.ds(0, (level + 1) * zrows), :], g_send.at[0])
            if level > 0:
                sent(w_all.at[pl.ds(0, (nz - level) * zrows), :], g_send.at[1])


def emit(dx_ref, dw_ref, dx_out, dw_out, sems):
    copies = [
        pltpu.make_async_copy(dx_ref, dx_out, sems.at[0]),
        pltpu.make_async_copy(dw_ref, dw_out, sems.at[1]),
    ]
    for copy in copies:
        copy.start()
    for copy in copies:
        copy.wait()


def fused(n, inputs, value_grad, value_weight, counts, offsets):
    tok, width = inputs.shape
    half = value_grad.shape[1]
    wfeat, wcols = value_weight.shape
    nz = n // GROUP
    fq = wfeat // GROUP
    hr = width // n // 2
    bf, f32, dma = jnp.bfloat16, jnp.float32, pltpu.SemaphoreType.DMA
    normalizer = 1.0 / math.sqrt(counts.shape[1] * n)
    vmem = pl.BlockSpec(memory_space=pltpu.VMEM)
    hbm = pl.BlockSpec(memory_space=pltpu.HBM)
    held = pl.pallas_call(
        functools.partial(kernel, n, normalizer),
        out_shape=(pltpu.VMEM((tok, wfeat), bf), pltpu.VMEM((2 * hr, half), f32)),
        in_specs=[hbm] * 5,
        out_specs=(vmem, vmem),
        scratch_shapes=[
            pltpu.SMEM(counts.shape, jnp.int32),
            pltpu.SMEM(offsets.shape, jnp.int32),
            pltpu.VMEM((tok, half), bf),
            pltpu.VMEM((wcols, wfeat), bf),
            pltpu.VMEM((nz, GROUP - 1, tok, hr), bf),
            pltpu.VMEM((2, GROUP * tok, half), bf),
            pltpu.VMEM((nz, GROUP * tok, 2 * hr), bf),
            pltpu.VMEM((n * wcols, fq), bf),
            pltpu.VMEM((GROUP * tok, fq), f32),
            pltpu.VMEM((nz, 2 * hr, half), f32),
            pltpu.VMEM((nz, 2 * hr, half), bf),
            pltpu.VMEM((nz + 1, 2 * hr, half), bf),
            pltpu.VMEM((GROUP - 1, tok, fq), bf),
            dma((7,)),
            dma, dma((GROUP - 1,)),
            dma, dma((4,)),
            dma, dma,
            dma, dma((nz,)),
            dma, dma((nz,)),
            dma((2,)), dma((nz, GROUP)),
            dma, dma((nz + 1, LANES)),
            dma, dma,
        ],
        compiler_params=pltpu.CompilerParams(
            collective_id=0, has_side_effects=True, vmem_limit_bytes=VMEM_ROOM
        ),
    )(counts, offsets, inputs, value_grad, value_weight.T)
    return pl.pallas_call(
        emit,
        out_shape=(
            jax.ShapeDtypeStruct((tok, wfeat), bf),
            jax.ShapeDtypeStruct((2 * hr, half), f32),
        ),
        in_specs=[vmem] * 2,
        out_specs=(hbm, hbm),
        scratch_shapes=[dma((2,))],
    )(*[pltpu.with_memory_space_constraint(part, pltpu.VMEM) for part in held])


def solution(mesh):
    n, tp = mesh.shape["fsdp"], mesh.shape["tp"]

    def local(inputs, value_grad, value_weight, counts, offsets):
        hr = inputs.shape[1] // n // 2
        fits = tp == 2 and n % (2 * GROUP) == 0 and n > 2 * GROUP and hr % 128 == 0
        fits = fits and value_weight.shape[1] % 16 == 0 and inputs.shape[0] % 32 == 0
        if fits:
            return fused(n, inputs, value_grad, value_weight, counts, offsets)
        return general(inputs, value_grad, value_weight, counts, offsets)

    in_specs = (P("fsdp", None), P("fsdp", "tp"), P("tp", "fsdp"), P("fsdp", None), P("fsdp", None))
    out_specs = (P("fsdp", "tp"), P("fsdp", "tp"))
    return jax.shard_map(local, mesh=mesh, in_specs=in_specs, out_specs=out_specs, check_vma=False)
```

time: 45.3 us -> 42.8 us (0.945)
  Pallas kernels: 44.5 us -> 42 us
    pallas_call x1, Pallas kernels: 43.3 us -> 40.8 us  [fused(): pl.pallas_call(functools.partial(kernel, n, normalizer), out_shape=(pltpu...]
where the time goes in v2:
time: 42.8 us; the launch traced here: 42.6 us
  Pallas kernels  42 us (98%)
  between operations  0.64 us (1%)
    pallas_call x1, Pallas kernels, fused(): pl.pallas_call(functools.partial(kernel, n, normalizer), out_shape=(pltpu...  40.8 us
    pallas_call x1, Pallas kernels, fused(): pl.pallas_call(emit, out_shape=(jax.ShapeDtypeStruct((tok, wfeat), bf), j...  1.16 us

profile of v2, /device:TPU:0, one launch (start us, length us, event | category | flops | bytes accessed | tf_op | source)
XLA Modules:
  0.0 42.6 jit_solution(11323235157684021102)
XLA Ops:
  0.6 40.8 %shard_map.68 = (bf16[256,2048]{1,0:T(8,128)(2,1)S(1)}, f32[256,512]{1,0:T(8,128)S(1)}) custom-call(s32[1,4]{1,0:T(1,128)} %counts_hbm.1, s32[1,4]{1,0:T(1,128)} %offsets_hbm.1, bf16[256,4096]{1,0:T(8,128)(2,1)} %x_hbm.1, bf16[256,512]{1,0:T(8,128)(2,1)} %g_hbm.1, bf16[64,2048]{1,0:T(8,128)(2,1)} %bitcast.1), custom_call_target="tpu_custom_call" | custom-call | tf_op jit(solution)/shard_map/pallas_call | solution.py:373
  41.5 1.2 %shard_map.69 = (bf16[256,2048]{1,0:T(8,128)(2,1)}, f32[256,512]{1,0:T(8,128)}) custom-call(bf16[256,2048]{1,0:T(8,128)(2,1)S(1)} %get-tuple-element.4.dx_ref, f32[256,512]{1,0:T(8,128)S(1)} %get-tuple-element.5.dw_ref), custom_call_target="tpu_custom_call" | custom-call | tf_op jit(solution)/shard_map/pallas_call | solution.py:406

commit v3 on v2

--- a/solution.py
+++ b/solution.py
@@ -11,6 +11,7 @@
 MESH = pl.DeviceIdType.MESH
 GROUP = 4
 LANES = 4
+CHUNKS = 8
 VMEM_ROOM = 54 * 2**20
 
 
@@ -65,7 +66,7 @@
     n, normalizer, counts_hbm, offsets_hbm, x_hbm, g_hbm, wt_hbm, dx_ref, dw_ref,
     counts_ref, offsets_ref, g_ref, wt_ref, x_src, s_all, x_all, w_all, acc, part_own, part_out, part_in,
     dx_out, local_sem, w_send, w_recv, s_send, s_recv, c_send, c_recv, x_send, x_recv,
-    xs_send, xs_recv, g_send, g_recv, p_send, p_recv, o_send, o_recv,
+    xs_send, xs_recv, g_send, g_recv, p_send, p_recv, o_send, o_recv, ready,
 ):
     nz = n // GROUP
     me = lax.axis_index("fsdp")
@@ -86,16 +87,14 @@
     order = [a + upper * (nz - 1 - 2 * a) for a in
              list(range(nz - 1, nz // 2 - 1, -1)) + list(range(nz // 2))]
     ways = ((0, 1, z < nz - 1, z > 0), (1, -1, z > 0, z < nz - 1))
-    inner = (z > 0) & (z < nz - 1)
-
     barrier = pltpu.get_barrier_semaphore()
     for j in range(1, GROUP):
         pl.semaphore_signal(barrier, inc=1, device_id=(me + steps[j], core), device_id_type=MESH)
     pl.semaphore_signal(barrier, inc=1, device_id=(me, sib), device_id_type=MESH)
-    for side, way, onward, behind in ways:
-        @pl.when(onward)
-        def _():
-            pl.semaphore_signal(barrier, inc=1, device_id=(me + GROUP * way, core), device_id_type=MESH)
+
+    @pl.when(z < nz - 1)
+    def _():
+        pl.semaphore_signal(barrier, inc=1, device_id=(me + GROUP, core), device_id_type=MESH)
 
     def remote(src, dst, send, recv, dev):
         return pltpu.make_async_remote_copy(
@@ -141,15 +140,15 @@
         pltpu.make_async_copy(x_hbm.at[:, block_lanes], x_all.at[i, slot(0), :], local_sem.at[6]).start()
 
     fetch_w.wait()
-    fetch_own.wait()
-
-    @pl.when(inner)
-    def _():
-        pl.semaphore_wait(barrier, GROUP + 2)
-
-    @pl.when(jnp.logical_not(inner))
+
+    @pl.when(z > 0)
     def _():
         pl.semaphore_wait(barrier, GROUP + 1)
+        pl.semaphore_signal(ready, inc=1, device_id=(me - GROUP, core), device_id_type=MESH)
+
+    @pl.when(z == 0)
+    def _():
+        pl.semaphore_wait(barrier, GROUP)
 
     for j in (3, 1, 2):
         remote(wt_ref.at[:, lanes((quarter + steps[j]) * fq, fq)], w_all.at[w_rows(me), :],
@@ -179,7 +178,11 @@
                 for j in range(GROUP):
                     chain(origin, -way, j).wait_recv()
 
-    chain_pass(0, 0)
+    fetch_own.wait()
+
+    @pl.when(z > 0)
+    def _():
+        chain(z, -1, 0).start()
 
     for fetch in (fetch_g, fetch_counts, fetch_offsets):
         fetch.wait()
@@ -219,6 +222,12 @@
 
     pltpu.make_async_copy(x_src, x_src, local_sem.at[5]).wait()
     x_start(0)
+
+    @pl.when(z < nz - 1)
+    def _():
+        pl.semaphore_wait(ready, 1)
+        chain(z, 1, 0).start()
+
     for j in (2, 3, 1):
         received(w_all.at[w_rows(me), :], w_recv.at[j - 1])
         chain_pass(0, j)
@@ -279,11 +288,11 @@
 
     pltpu.make_async_copy(x_all.at[:, slot(0), :], x_all.at[:, slot(0), :], local_sem.at[6]).wait()
     x_swap(0)
-    received(x_all.at[0, others, mine], xs_recv.at[0])
-    part_own[order[0]] = contract(0, pl.ds(0, (GROUP - 1) * tok))
     for k in range(2, nz):
         for j in (0, 2, 3, 1):
             chain_pass(k, j)
+    received(x_all.at[0, others, mine], xs_recv.at[0])
+    part_own[order[0]] = contract(0, pl.ds(0, (GROUP - 1) * tok))
     received(s_all.at[core, pl.ds(0, 2 * hop), :], s_recv.at[3])
     to_core(3, 1)
     part_own[order[0]] = part_own[order[0]] + contract(0, slot(GROUP - 1))
@@ -295,29 +304,51 @@
     far = pl.ds(pl.multiple_of((1 - upper) * half, half), half)
     for j in range(GROUP):
         acc[slot(j), :] = jnp.dot(s_all[upper, slot(j), :], w_all[near, :], preferred_element_type=jnp.float32)
-    block(1)
-    for k in range(2, nz):
-        chain_end(k)
+
     own_lanes = lanes(quarter * fq, fq)
     first = jnp.where(quarter == 1, 1, GROUP - 1)
-    for j, step in ((first, jnp.where(quarter == 1, steps[1], steps[3])),
-                    (GROUP - first, jnp.where(quarter == 1, steps[3], steps[1])),
-                    (2, steps[2]), (0, None)):
-        rows = pl.ds(pl.multiple_of(j * tok, tok), tok)
-        product = acc[rows, :] + jnp.dot(
-            s_all[1 - upper, rows, :], w_all[far, :], preferred_element_type=jnp.float32)
-        if step is None:
-            dx_ref[:, own_lanes] = product.astype(jnp.bfloat16)
-        else:
-            dx_out[j - 1] = product.astype(jnp.bfloat16)
-            remote(dx_out.at[j - 1], dx_ref.at[:, own_lanes], o_send, o_recv, (me + step, core)).start()
+
+    def give():
+        for k in range(2, nz):
+            chain_end(k)
+        for j, step in ((first, jnp.where(quarter == 1, steps[1], steps[3])),
+                        (2, steps[2]),
+                        (GROUP - first, jnp.where(quarter == 1, steps[3], steps[1])), (0, None)):
+            rows = pl.ds(pl.multiple_of(j * tok, tok), tok)
+            product = acc[rows, :] + jnp.dot(
+                s_all[1 - upper, rows, :], w_all[far, :], preferred_element_type=jnp.float32)
+            if step is None:
+                dx_ref[:, own_lanes] = product.astype(jnp.bfloat16)
+            else:
+                dx_out[j - 1] = product.astype(jnp.bfloat16)
+                remote(dx_out.at[j - 1], dx_ref.at[:, own_lanes], o_send, o_recv, (me + step, core)).start()
+
+    between = (z > 0) & (z < nz - 1)
+
+    @pl.when(between & (core == 0))
+    def _():
+        give()
 
     for lane in range(LANES):
         forward(0, lane)
-    for i in range(2, nz):
+    block(1)
+
+    @pl.when(jnp.logical_not(between))
+    def _():
+        give()
+
+    block(2)
+
+    @pl.when(between & (core == 1))
+    def _():
+        give()
+
+    for lane in range(LANES):
+        forward(2, lane)
+        forward(1, lane)
+    for i in range(3, nz):
         block(i)
-    for lane in range(LANES):
-        for i in list(range(2, nz)) + [1]:
+        for lane in range(LANES):
             forward(i, lane)
 
     for lane in range(LANES):
@@ -349,14 +380,13 @@
 
 
 def emit(dx_ref, dw_ref, dx_out, dw_out, sems):
-    copies = [
-        pltpu.make_async_copy(dx_ref, dx_out, sems.at[0]),
-        pltpu.make_async_copy(dw_ref, dw_out, sems.at[1]),
-    ]
-    for copy in copies:
-        copy.start()
-    for copy in copies:
-        copy.wait()
+    for src, dst, sem in ((dx_ref, dx_out, sems.at[0]), (dw_ref, dw_out, sems.at[1])):
+        rows = src.shape[0] // CHUNKS
+        for i in range(CHUNKS):
+            part = pl.ds(i * rows, rows)
+            pltpu.make_async_copy(src.at[part, :], dst.at[part, :], sem).start()
+    pltpu.make_async_copy(dx_ref, dx_out, sems.at[0]).wait()
+    pltpu.make_async_copy(dw_ref, dw_out, sems.at[1]).wait()
 
 
 def fused(n, inputs, value_grad, value_weight, counts, offsets):
@@ -398,6 +428,7 @@
             dma((2,)), dma((nz, GROUP)),
             dma, dma((nz + 1, LANES)),
             dma, dma,
+            pltpu.SemaphoreType.REGULAR,
         ],
         compiler_params=pltpu.CompilerParams(
             collective_id=0, has_side_effects=True, vmem_limit_bytes=VMEM_ROOM

time: 42.8 us -> 41.6 us (0.972)
  Pallas kernels: 42 us -> 40.8 us
    pallas_call x1, Pallas kernels: 40.8 us -> 39.7 us  [fused(): pl.pallas_call(functools.partial(kernel, n, normalizer), out_shape=(pltpu...]
where the time goes in v3:
time: 41.6 us; the launch traced here: 41.4 us
  Pallas kernels  40.8 us (98%)
  between operations  0.64 us (2%)
    pallas_call x1, Pallas kernels, fused(): pl.pallas_call(functools.partial(kernel, n, normalizer), out_shape=(pltpu...  39.7 us
    pallas_call x1, Pallas kernels, fused(): pl.pallas_call(emit, out_shape=(jax.ShapeDtypeStruct((tok, wfeat), bf), j...  1.14 us

profile of v3, /device:TPU:0, one launch (start us, length us, event | category | flops | bytes accessed | tf_op | source)
XLA Modules:
  0.0 41.4 jit_solution(2268739393503901248)
XLA Ops:
  0.6 39.7 %shard_map.68 = (bf16[256,2048]{1,0:T(8,128)(2,1)S(1)}, f32[256,512]{1,0:T(8,128)S(1)}) custom-call(s32[1,4]{1,0:T(1,128)} %counts_hbm.1, s32[1,4]{1,0:T(1,128)} %offsets_hbm.1, bf16[256,4096]{1,0:T(8,128)(2,1)} %x_hbm.1, bf16[256,512]{1,0:T(8,128)(2,1)} %g_hbm.1, bf16[64,2048]{1,0:T(8,128)(2,1)} %bitcast.1), custom_call_target="tpu_custom_call" | custom-call | tf_op jit(solution)/shard_map/pallas_call | solution.py:403
  40.3 1.1 %shard_map.69 = (bf16[256,2048]{1,0:T(8,128)(2,1)}, f32[256,512]{1,0:T(8,128)}) custom-call(bf16[256,2048]{1,0:T(8,128)(2,1)S(1)} %get-tuple-element.4.dx_ref, f32[256,512]{1,0:T(8,128)S(1)} %get-tuple-element.5.dw_ref), custom_call_target="tpu_custom_call" | custom-call | tf_op jit(solution)/shard_map/pallas_call | solution.py:437

commit v4 on v3

--- a/solution.py
+++ b/solution.py
@@ -199,15 +199,16 @@
 
     hop = tok // 2
 
-    def s_send_rows(j, src_slot, dst_slot, h, sem, onto):
-        first = ((j - 1 + h) % 2) * hop
-        remote(s_all.at[core, pl.ds(src_slot * tok + first, hop), :],
-               s_all.at[core, pl.ds(dst_slot * tok + first, hop), :],
+    spared = hop // 4
+
+    def s_send_rows(src_slot, dst_slot, first, count, sem, onto):
+        remote(s_all.at[core, pl.ds(src_slot * tok + first, count), :],
+               s_all.at[core, pl.ds(dst_slot * tok + first, count), :],
                s_send, s_recv.at[sem], (me + steps[onto], core)).start()
 
     for h in range(2):
         for j in (1, 2):
-            s_send_rows(j, 0, j, h, 2 if h else j - 1, j)
+            s_send_rows(0, j, ((j - 1 + h) % 2) * hop, hop, 2 if h else j - 1, j)
 
     def to_core(first, count):
         rows = pl.ds(first * tok, count * tok)
@@ -231,14 +232,30 @@
     for j in (2, 3, 1):
         received(w_all.at[w_rows(me), :], w_recv.at[j - 1])
         chain_pass(0, j)
-    for j, onto in ((1, 2), (2, 1)):
-        received(s_all.at[core, pl.ds(0, hop), :], s_recv.at[j - 1])
-        s_send_rows(j, j, 3, 0, 3, onto)
-    for i in range(1, nz):
-        x_start(i)
+    received(s_all.at[core, pl.ds(0, hop), :], s_recv.at[0])
+    s_send_rows(1, 3, 0, hop - spared, 3, 2)
+
+    @pl.when(me != 2)
+    def _():
+        s_send_rows(1, 3, hop - spared, spared, 3, 2)
+
+    received(s_all.at[core, pl.ds(0, hop), :], s_recv.at[1])
+    s_send_rows(2, 3, hop, hop, 3, 1)
+    @pl.when(me != 1)
+    def _():
+        for i in range(1, nz):
+            x_start(i)
+
     for j in (0, 2, 3, 1):
         chain_pass(1, j)
     received(s_all.at[core, pl.ds(0, 2 * hop), :], s_recv.at[2])
+
+    @pl.when(me == 1)
+    def _():
+        s_send_rows(2, 3, hop - spared, spared, 3, 1)
+        for i in range(1, nz):
+            x_start(i)
+
     to_core(1, 2)
 
     def partial_copy(t, side, lane, way, target):
@@ -325,7 +342,9 @@
 
     between = (z > 0) & (z < nz - 1)
 
-    @pl.when(between & (core == 0))
+    early = (between & (core == 0)) | ((z == 0) & (core == 1))
+
+    @pl.when(early)
     def _():
         give()
 
@@ -333,7 +352,7 @@
         forward(0, lane)
     block(1)
 
-    @pl.when(jnp.logical_not(between))
+    @pl.when(jnp.logical_not(between | early))
     def _():
         give()
 
@@ -364,7 +383,19 @@
     received(dx_out, o_recv)
 
     sent(w_all.at[pl.ds(0, (GROUP - 1) * wcols), :], w_send)
-    sent(s_all.at[0, others, :], s_send)
+
+    @pl.when(me == 1)
+    def _():
+        sent(s_all.at[0, pl.ds(0, 3 * tok + spared), :], s_send)
+
+    @pl.when(me == 2)
+    def _():
+        sent(s_all.at[0, pl.ds(0, 3 * tok - spared), :], s_send)
+
+    @pl.when((me != 1) & (me != 2))
+    def _():
+        sent(s_all.at[0, others, :], s_send)
+
     sent(s_all.at[0], c_send)
     sent(x_src, x_send)
     sent(x_all.at[:, others, mine], xs_send)

time: 41.6 us -> 41 us (0.986)
  Pallas kernels: 40.8 us -> 40.2 us
    pallas_call x1, Pallas kernels: 39.7 us -> 39.1 us  [fused(): pl.pallas_call(functools.partial(kernel, n, normalizer), out_shape=(pltpu...]
where the time goes in v4:
time: 41 us; the launch traced here: 40.9 us
  Pallas kernels  40.2 us (98%)
  between operations  0.64 us (2%)
    pallas_call x1, Pallas kernels, fused(): pl.pallas_call(functools.partial(kernel, n, normalizer), out_shape=(pltpu...  39.1 us
    pallas_call x1, Pallas kernels, fused(): pl.pallas_call(emit, out_shape=(jax.ShapeDtypeStruct((tok, wfeat), bf), j...  1.14 us

profile of v4, /device:TPU:0, one launch (start us, length us, event | category | flops | bytes accessed | tf_op | source)
XLA Modules:
  0.0 40.9 jit_solution(18086940263327111374)
XLA Ops:
  0.6 39.1 %shard_map.68 = (bf16[256,2048]{1,0:T(8,128)(2,1)S(1)}, f32[256,512]{1,0:T(8,128)S(1)}) custom-call(s32[1,4]{1,0:T(1,128)} %counts_hbm.1, s32[1,4]{1,0:T(1,128)} %offsets_hbm.1, bf16[256,4096]{1,0:T(8,128)(2,1)} %x_hbm.1, bf16[256,512]{1,0:T(8,128)(2,1)} %g_hbm.1, bf16[64,2048]{1,0:T(8,128)(2,1)} %bitcast.1), custom_call_target="tpu_custom_call" | custom-call | tf_op jit(solution)/shard_map/pallas_call | solution.py:434
  39.7 1.1 %shard_map.69 = (bf16[256,2048]{1,0:T(8,128)(2,1)}, f32[256,512]{1,0:T(8,128)}) custom-call(bf16[256,2048]{1,0:T(8,128)(2,1)S(1)} %get-tuple-element.4.dx_ref, f32[256,512]{1,0:T(8,128)S(1)} %get-tuple-element.5.dw_ref), custom_call_target="tpu_custom_call" | custom-call | tf_op jit(solution)/shard_map/pallas_call | solution.py:468

commit v5 on v4

--- a/solution.py
+++ b/solution.py
@@ -370,6 +370,31 @@
         for lane in range(LANES):
             forward(i, lane)
 
+    sent(w_all.at[pl.ds(0, (GROUP - 1) * wcols), :], w_send)
+
+    @pl.when(me == 1)
+    def _():
+        sent(s_all.at[0, pl.ds(0, 3 * tok + spared), :], s_send)
+
+    @pl.when(me == 2)
+    def _():
+        sent(s_all.at[0, pl.ds(0, 3 * tok - spared), :], s_send)
+
+    @pl.when((me != 1) & (me != 2))
+    def _():
+        sent(s_all.at[0, others, :], s_send)
+
+    sent(s_all.at[0], c_send)
+    sent(x_src, x_send)
+    sent(x_all.at[:, others, mine], xs_send)
+    for level in range(nz):
+        @pl.when(z == level)
+        def _():
+            if level < nz - 1:
+                sent(w_all.at[pl.ds(0, (level + 1) * zrows), :], g_send.at[0])
+            if level > 0:
+                sent(w_all.at[pl.ds(0, (nz - level) * zrows), :], g_send.at[1])
+
     for lane in range(LANES):
         rows = pl.ds(lane * lane_rows, lane_rows)
         for side, way, onward, behind in ways:
@@ -380,34 +405,10 @@
                 part_own[z, rows, :] = part_own[z, rows, :] + part_in[place, rows, :].astype(jnp.float32)
         dw_ref[rows, :] = part_own[z, rows, :] * normalizer
 
+    sent(part_out.at[pl.ds(0, nz - 1)], p_send)
     received(dx_out, o_recv)
 
-    sent(w_all.at[pl.ds(0, (GROUP - 1) * wcols), :], w_send)
-
-    @pl.when(me == 1)
-    def _():
-        sent(s_all.at[0, pl.ds(0, 3 * tok + spared), :], s_send)
-
-    @pl.when(me == 2)
-    def _():
-        sent(s_all.at[0, pl.ds(0, 3 * tok - spared), :], s_send)
-
-    @pl.when((me != 1) & (me != 2))
-    def _():
-        sent(s_all.at[0, others, :], s_send)
-
-    sent(s_all.at[0], c_send)
-    sent(x_src, x_send)
-    sent(x_all.at[:, others, mine], xs_send)
     sent(dx_out, o_send)
-    sent(part_out.at[pl.ds(0, nz - 1)], p_send)
-    for level in range(nz):
-        @pl.when(z == level)
-        def _():
-            if level < nz - 1:
-                sent(w_all.at[pl.ds(0, (level + 1) * zrows), :], g_send.at[0])
-            if level > 0:
-                sent(w_all.at[pl.ds(0, (nz - level) * zrows), :], g_send.at[1])
 
 
 def emit(dx_ref, dw_ref, dx_out, dw_out, sems):

time: 41 us -> 41 us (level)
  no operation moved by 1% of the time
where the time goes in v5:
time: 41 us; the launch traced here: 40.9 us
  Pallas kernels  40.2 us (98%)
  between operations  0.64 us (2%)
    pallas_call x1, Pallas kernels, fused(): pl.pallas_call(functools.partial(kernel, n, normalizer), out_shape=(pltpu...  39.1 us
    pallas_call x1, Pallas kernels, fused(): pl.pallas_call(emit, out_shape=(jax.ShapeDtypeStruct((tok, wfeat), bf), j...  1.14 us

profile of v5, /device:TPU:0, one launch (start us, length us, event | category | flops | bytes accessed | tf_op | source)
XLA Modules:
  0.0 40.9 jit_solution(17035535514437585771)
XLA Ops:
  0.6 39.1 %shard_map.68 = (bf16[256,2048]{1,0:T(8,128)(2,1)S(1)}, f32[256,512]{1,0:T(8,128)S(1)}) custom-call(s32[1,4]{1,0:T(1,128)} %counts_hbm.1, s32[1,4]{1,0:T(1,128)} %offsets_hbm.1, bf16[256,4096]{1,0:T(8,128)(2,1)} %x_hbm.1, bf16[256,512]{1,0:T(8,128)(2,1)} %g_hbm.1, bf16[64,2048]{1,0:T(8,128)(2,1)} %bitcast.1), custom_call_target="tpu_custom_call" | custom-call | tf_op jit(solution)/shard_map/pallas_call | solution.py:435
  39.7 1.1 %shard_map.69 = (bf16[256,2048]{1,0:T(8,128)(2,1)}, f32[256,512]{1,0:T(8,128)}) custom-call(bf16[256,2048]{1,0:T(8,128)(2,1)S(1)} %get-tuple-element.4.dx_ref, f32[256,512]{1,0:T(8,128)S(1)} %get-tuple-element.5.dw_ref), custom_call_target="tpu_custom_call" | custom-call | tf_op jit(solution)/shard_map/pallas_call | solution.py:469
